TPU v7x, 32 devices: a whole 2x2x4 slice. The times are simulated.
32 devices in a mesh: grp: 4 (over y, x), dom: 8 (over z, core).
Axes of the slice: x: 2, y: 2, z: 4, core: 2. Of those that a mesh axis runs over, the one named last changes fastest.
Arguments:
- node_state: float32 [4096, 6, 128], P(('grp', 'dom')), may hold values from -6 to 6
- node_dest: int32 [4096], P(('grp', 'dom')), may hold values from 0 to 7, as said below
- seg_nodes: float32 [6, 16384], P(None, ('grp', 'dom')), may hold values from -6 to 6
- seg_conn: int32 [3, 32768], P(None, ('grp', 'dom')), may hold values from 0 to 511
- pair_seg: int32 [32, 4, 32], P(('grp', 'dom')), may hold values from 0 to 7
- pair_slot: int32 [32, 4, 32], P(('grp', 'dom')), may hold values from 0 to 255, as said below
Outputs:
- node_force: float32 [4096, 3, 128], P(('grp', 'dom'))
Inputs may be any that keep to these rules, and one draw needn't show every extreme that they name: `node_dest`: at most 32 blocks of one device name the same contact domain; in every grp row one contact domain receives exactly 32 blocks from every device of that row; every device sends at least one block to the contact domain of its own dom index. `pair_slot`: every entry names a slot d * 32 + k that holds a block: device (r, d) sends more than k blocks to the contact domain.
All inputs are finite; a program needn't handle non-finite values.
Results may differ from a plain program's by a relative error of at most 0.00023.
Values sent between devices are 32-bit elements; how exact they have to be, the bound alone decides.
A program may use at most 64 MiB of HBM per device.

v0:
```python
import jax
import jax.numpy as jnp
from jax import lax
from jax.sharding import PartitionSpec as P

SEG_BLK = 128
time_step = 0.5
stiffness = 0.5
radius_sq = 0.5


def seg_geometry(corners):
    corner_a = corners[:, 0]
    corner_b = corners[:, 1]
    corner_c = corners[:, 2]
    edge_one = corner_b[0:3] - corner_a[0:3]
    edge_two = corner_c[0:3] - corner_a[0:3]
    normal = 0.5 * jnp.stack(
        [
            edge_one[1] * edge_two[2] - edge_one[2] * edge_two[1],
            edge_one[2] * edge_two[0] - edge_one[0] * edge_two[2],
            edge_one[0] * edge_two[1] - edge_one[1] * edge_two[0],
        ]
    )
    centre = (corner_a[0:3] + corner_b[0:3] + corner_c[0:3]) / 3.0
    motion = (corner_a[3:6] + corner_b[3:6] + corner_c[3:6]) / 3.0
    return jnp.concatenate([normal, centre, motion], axis=0)


def tile_force(node_rows, geometry):
    clearance = jnp.zeros((geometry.shape[1], node_rows.shape[1]), jnp.float32)
    distance = jnp.zeros((geometry.shape[1], node_rows.shape[1]), jnp.float32)
    for axis_id in range(3):
        offset = node_rows[axis_id][None, :] - geometry[3 + axis_id][:, None]
        drift = node_rows[3 + axis_id][None, :] - geometry[6 + axis_id][:, None]
        clearance = clearance + geometry[axis_id][:, None] * (offset + time_step * drift)
        distance = distance + offset * offset
    pressure = stiffness * jnp.exp(-distance / radius_sq) * jnp.maximum(-clearance, 0.0)
    return jnp.dot(
        geometry[0:3], pressure, precision=lax.Precision.HIGHEST, preferred_element_type=jnp.float32
    )


def place_rows(slot_ids, values, slot_total):
    onehot = (slot_ids[None, :] == jnp.arange(slot_total, dtype=jnp.int32)[:, None]).astype(
        jnp.float32
    )
    flattened = values.reshape(values.shape[0], -1)
    placed = jnp.dot(
        onehot, flattened, precision=lax.Precision.HIGHEST, preferred_element_type=jnp.float32
    )
    return placed.reshape((slot_total,) + values.shape[1:])


def shards(node_state, node_dest, seg_nodes, seg_conn, pair_seg, pair_slot):
    dom_count = lax.axis_size("dom")
    grp_count = lax.axis_size("grp")
    block_count = node_state.shape[0]
    capacity = max(2, 2 * block_count // dom_count)
    slot_count = dom_count * capacity
    order_ids = jnp.arange(block_count, dtype=jnp.int32)
    earlier = order_ids[None, :] < order_ids[:, None]
    same_dom = node_dest[:, None] == node_dest[None, :]
    slot_rank = jnp.sum((same_dom & earlier).astype(jnp.int32), axis=1)
    target_slot = node_dest * capacity + slot_rank
    outgoing = place_rows(target_slot, node_state, slot_count)
    received = lax.all_to_all(outgoing, "dom", split_axis=0, concat_axis=0, tiled=True)
    corners = jnp.take(seg_nodes, seg_conn, axis=1)
    geometry = seg_geometry(corners)
    seg_blocks = geometry.shape[1] // SEG_BLK
    geo_blocks = jnp.transpose(geometry.reshape(9, seg_blocks, SEG_BLK), (1, 0, 2))
    seg_table = pair_seg[0]
    slot_table = pair_slot[0]
    geo_all = lax.all_gather(geo_blocks, "grp", axis=0, tiled=True)
    seg_in, slot_in = (
        lax.all_to_all(seg_table, "grp", split_axis=0, concat_axis=0, tiled=True),
        lax.all_to_all(slot_table, "grp", split_axis=0, concat_axis=0, tiled=True),
    )
    owner_base = (jnp.arange(grp_count, dtype=jnp.int32) * seg_blocks)[:, None]
    seg_ids = (seg_in + owner_base).reshape(-1)
    slot_ids = slot_in.reshape(-1)
    forces = jax.vmap(tile_force)(
        jnp.take(received, slot_ids, axis=0), jnp.take(geo_all, seg_ids, axis=0)
    )
    own_forces = place_rows(slot_ids, forces, slot_count)
    returned = lax.all_to_all(own_forces, "dom", split_axis=0, concat_axis=0, tiled=True)
    return jnp.take(returned, target_slot, axis=0)


def solution(mesh):
    in_specs = (
        P(("grp", "dom"), None, None),
        P(("grp", "dom")),
        P(None, ("grp", "dom")),
        P(None, ("grp", "dom")),
        P(("grp", "dom"), None, None),
        P(("grp", "dom"), None, None),
    )
    out_specs = P(("grp", "dom"), None, None)
    return jax.shard_map(shards, mesh=mesh, in_specs=in_specs, out_specs=out_specs, check_vma=False)
```

profile of v0, /device:TPU:0, one launch (start us, length us, event | category | flops | bytes accessed | tf_op | source)
XLA Modules:
  0.0 130.9 jit_solution(8303364324702544644)
XLA Ops:
  0.0 5.2 %all-to-all-start.1 = ((s32[4,1,32]{2,1,0:T(1,128)}), s32[4,1,32]{2,1,0:T(1,128)S(1)}, u32[]{:S(2)}, u32[]{:S(2)}) async-start(s32[4,1,32]{2,1,0:T(1,128)} %bitcast.88), calls=%async_computation.1 | async-start | bytes 4096 | tf_op jit(solution)/shard_map/all_to_all | solution.py:76
  5.2 0.7 compare_and_fusion
  5.9 0.7 compare_select_fusion
  6.7 0.9 convert_reduce_fusion
  7.6 0.7 compare_and_fusion.3
  8.3 0.9 copy.46
  9.1 1.2 copy.49
  10.3 8.1 %gather_fusion = f32[3072,6]{1,0:T(8,128)S(1)} fusion(f32[6,512]{0,1:T(8,128)S(1)} %copy.46, s32[3072]{0:T(1024)S(1)} %broadcast_clamp_fusion), kind=kCustom, calls=%fused_computation | custom fusion | bytes 159744 | tf_op jit(solution)/shard_map/jit(_take)/gather | solution.py:68
  18.4 0.5 copy.47
  19.0 0.5 fusion.34
  19.6 9.6 %all_gather.3 = f32[32,9,128]{2,0,1:T(8,128)S(1)} all-gather(f32[8,9,128]{2,0,1:T(8,128)S(1)} %maximum_bitcast_fusion), channel_id=1, replica_groups=mesh['grp'=4,'dom'=8] {'grp'}, dimensions={0}, use_global_device_ids=true | all-gather | bytes 184320 | tf_op jit(solution)/shard_map/all_gather | solution.py:74
  29.4 1.4 %copy.50 = f32[256,6,128]{2,1,0:T(8,128)} copy(f32[256,6,128]{2,0,1:T(8,128)S(1)} %fusion.34) | data formatting | bytes 1572864 | tf_op jit(solution)/shard_map/dot_general | solution.py:49
  30.9 3.2 %all-to-all-start = ((s32[4,1,32]{2,1,0:T(1,128)}), s32[4,1,32]{2,1,0:T(1,128)S(1)}, u32[]{:S(2)}, u32[]{:S(2)}) async-start(s32[4,1,32]{2,1,0:T(1,128)} %bitcast.1), calls=%async_computation | async-start | bytes 4096 | tf_op jit(solution)/shard_map/all_to_all | solution.py:77
  34.3 0.5 broadcast.128
  34.8 0.7 reduce.10
  35.5 3.1 %all-to-all-done = s32[4,1,32]{2,1,0:T(1,128)S(1)} async-done(((s32[4,1,32]{2,1,0:T(1,128)}), s32[4,1,32]{2,1,0:T(1,128)S(1)}, u32[]{:S(2)}, u32[]{:S(2)}) %all-to-all-start) | async-done | bytes 544 | tf_op jit(solution)/shard_map/all_to_all | solution.py:77
  38.7 4.9 %all-to-all-start.2 = ((f32[256,6,128]{2,1,0:T(8,128)}), f32[256,6,128]{2,1,0:T(8,128)S(1)}, u32[]{:S(2)}, u32[]{:S(2)}) async-start(f32[256,6,128]{2,1,0:T(8,128)} %copy.50), calls=%async_computation.2 | async-start | bytes 2097152 | tf_op jit(solution)/shard_map/all_to_all | solution.py:67
  43.6 0.7 reduce.11
  44.4 0.8 gather_fusion.1
  45.2 0.6 compare_and_fusion.1
  46.0 1.0 fusion.53
  47.0 23.1 %all-to-all-done.2 = f32[256,6,128]{2,1,0:T(8,128)S(1)} async-done(((f32[256,6,128]{2,1,0:T(8,128)}), f32[256,6,128]{2,1,0:T(8,128)S(1)}, u32[]{:S(2)}, u32[]{:S(2)}) %all-to-all-start.2) | async-done | bytes 786464 | tf_op jit(solution)/shard_map/all_to_all | solution.py:67
  70.1 0.8 gather_fusion.2
  71.1 0.3 fusion.54
  71.4 0.3 copy-done
  71.8 37.2 %fusion.14 = f32[128,3,128]{2,1,0:T(4,128)S(1)} fusion(f32[128,128]{1,0:T(8,128)S(1)} %bitcast.69, f32[128,128]{1,0:T(8,128)S(1)} %bitcast.78, f32[128,128]{1,0:T(8,128)S(1)} %bitcast.70, f32[128,128]{1,0:T(8,128)S(1)} %bitcast.71, f32[128,128]{1,0:T(8,128)S(1)} %bitcast.79, f32[128,128]{1,0:T(8,128)S(1)} %bitcast.72, f32[128,128]{1,0:T(8,128)S(1)} %bitcast.73, ...), kind=kOutput, calls=%fused_computation.24 | convolution fusion | flops 134217728 | bytes 1441792 | tf_op jit(solution)/shard_map/vmap()/dot_general | solution.py:39
  109.1 0.3 fusion.37
  109.4 1.1 copy.52
  110.5 3.5 %all-to-all-start.3 = ((f32[256,3,128]{2,1,0:T(4,128)}), f32[256,3,128]{2,1,0:T(4,128)S(1)}, u32[]{:S(2)}, u32[]{:S(2)}) async-start(f32[256,3,128]{2,1,0:T(4,128)} %copy.52), calls=%async_computation.3 | async-start | bytes 1048576 | tf_op jit(solution)/shard_map/all_to_all | solution.py:86
  114.0 15.2 %all-to-all-done.3 = f32[256,3,128]{2,1,0:T(4,128)S(1)} async-done(((f32[256,3,128]{2,1,0:T(4,128)}), f32[256,3,128]{2,1,0:T(4,128)S(1)}, u32[]{:S(2)}, u32[]{:S(2)}) %all-to-all-start.3) | async-done | bytes 393248 | tf_op jit(solution)/shard_map/all_to_all | solution.py:86
  129.3 0.8 gather_fusion.3
  130.2 0.7 copy.53
  (36 shorter events, 1.6 us)
Async XLA Ops:
  0.0 30.9 %all-to-all-start.1 = ((s32[4,1,32]{2,1,0:T(1,128)}), s32[4,1,32]{2,1,0:T(1,128)S(1)}, u32[]{:S(2)}, u32[]{:S(2)}) async-start(s32[4,1,32]{2,1,0:T(1,128)} %bitcast.88), calls=%async_computation.1 | async-start | bytes 4096 | tf_op jit(solution)/shard_map/all_to_all | solution.py:76
  30.9 7.8 %all-to-all-start = ((s32[4,1,32]{2,1,0:T(1,128)}), s32[4,1,32]{2,1,0:T(1,128)S(1)}, u32[]{:S(2)}, u32[]{:S(2)}) async-start(s32[4,1,32]{2,1,0:T(1,128)} %bitcast.1), calls=%async_computation | async-start | bytes 4096 | tf_op jit(solution)/shard_map/all_to_all | solution.py:77
  38.7 31.4 %all-to-all-start.2 = ((f32[256,6,128]{2,1,0:T(8,128)}), f32[256,6,128]{2,1,0:T(8,128)S(1)}, u32[]{:S(2)}, u32[]{:S(2)}) async-start(f32[256,6,128]{2,1,0:T(8,128)} %copy.50), calls=%async_computation.2 | async-start | bytes 2097152 | tf_op jit(solution)/shard_map/all_to_all | solution.py:67
  46.0 24.9 %copy-start.3 = (pred[128]{0:T(512)(128)(4,1)S(1)}, pred[128]{0:T(512)(128)(4,1)}, u32[]{:S(2)}) copy-start(pred[128]{0:T(512)(128)(4,1)} %compare_and_fusion.1) | copy-start | bytes 388
  70.9 0.8 copy-start
  70.9 0.9 copy-start.1
  70.9 0.9 copy-start.2
  110.5 18.8 %all-to-all-start.3 = ((f32[256,3,128]{2,1,0:T(4,128)}), f32[256,3,128]{2,1,0:T(4,128)S(1)}, u32[]{:S(2)}, u32[]{:S(2)}) async-start(f32[256,3,128]{2,1,0:T(4,128)} %copy.52), calls=%async_computation.3 | async-start | bytes 1048576 | tf_op jit(solution)/shard_map/all_to_all | solution.py:86
where the time goes:
time: 132 us; the launch traced here: 131 us
  waiting for transfers between devices  41.4 us (31%)
  matrix products  38 us (29%)
  local copies, waits for them, and re-layouts  19.1 us (14%)
  starting transfers between devices  16.8 us (13%)
  blocking collectives  9.62 us (7%)
  other arithmetic  5.68 us (4%)
    dot_general x1, matrix products, tile_force(): jnp.dot(geometry[0:3], pressure, precision=lax.Precision.HIGHEST, preferr...  37.2 us
    all_to_all x1, waiting for transfers between devices, shards(): lax.all_to_all(outgoing, 'dom', split_axis=0, concat_axis=0, tiled=True)  23.1 us
    all_to_all x1, waiting for transfers between devices, shards(): lax.all_to_all(own_forces, 'dom', split_axis=0, concat_axis=0, tiled=True)  15.2 us
    all_gather x1, blocking collectives, shards(): geo_all = lax.all_gather(geo_blocks, 'grp', axis=0, tiled=True)  9.62 us
    gather x2, local copies, waits for them, and re-layouts, shards(): corners = jnp.take(seg_nodes, seg_conn, axis=1)  8.61 us
    all_to_all x1, starting transfers between devices, shards(): lax.all_to_all(seg_table, 'grp', split_axis=0, concat_axis=0, tiled=True)  5.19 us
    all_to_all x1, starting transfers between devices, shards(): lax.all_to_all(outgoing, 'dom', split_axis=0, concat_axis=0, tiled=True)  4.88 us
    all_to_all x1, starting transfers between devices, shards(): lax.all_to_all(own_forces, 'dom', split_axis=0, concat_axis=0, tiled=True)  3.49 us
  transfers between devices with their start and end apart: 4, of which 3 were waited for; matrix products, arithmetic and copies ran while one was open for 16% of the time, Pallas kernels for 0%

commit v1 on v0

--- a/solution.py
+++ b/solution.py
@@ -7,6 +7,17 @@
 time_step = 0.5
 stiffness = 0.5
 radius_sq = 0.5
+
+
+def turned_line(x, name, d):
+    n_dev = lax.axis_size(name)
+    route = [(i, (i + 1) % n_dev) for i in range(n_dev)]
+    parts = [x]
+    for hop in range(1, n_dev):
+        parts = [lax.ppermute(parts[0], name, route), *parts]
+    full = jnp.concatenate(parts, axis=d)
+    shift = (lax.axis_index(name) + 1) * parts[-1].shape[d]
+    return jnp.roll(full, shift, axis=d)
 
 
 def seg_geometry(corners):
@@ -71,7 +82,7 @@
     geo_blocks = jnp.transpose(geometry.reshape(9, seg_blocks, SEG_BLK), (1, 0, 2))
     seg_table = pair_seg[0]
     slot_table = pair_slot[0]
-    geo_all = lax.all_gather(geo_blocks, "grp", axis=0, tiled=True)
+    geo_all = turned_line(geo_blocks, "grp", 0)
     seg_in, slot_in = (
         lax.all_to_all(seg_table, "grp", split_axis=0, concat_axis=0, tiled=True),
         lax.all_to_all(slot_table, "grp", split_axis=0, concat_axis=0, tiled=True),

time: 132 us -> 121 us (0.917)
  blocking collectives: 9.62 us -> 0 us
  starting transfers between devices: 16.8 us -> 19.4 us
  waiting for transfers between devices: 41.4 us -> 39.4 us
  local copies, waits for them, and re-layouts: 19.1 us -> 17.7 us
    all_to_all x1, waiting for transfers between devices: 23.1 us -> 12.4 us  [shards(): lax.all_to_all(outgoing, 'dom', split_axis=0, concat_axis=0, tiled=True)]
    ppermute x0 -> x3, waiting for transfers between devices: none -> 9.98 us  [turned_line(): parts = [lax.ppermute(parts[0], name, route), *parts]]
    all_gather x1 -> x0, blocking collectives: 9.62 us -> none  [shards(): geo_all = lax.all_gather(geo_blocks, 'grp', axis=0, tiled=True)]
    ppermute x0 -> x3, starting transfers between devices: none -> 2.65 us  [turned_line(): parts = [lax.ppermute(parts[0], name, route), *parts]]
    all_to_all x1, waiting for transfers between devices: 3.12 us -> 1.77 us  [shards(): lax.all_to_all(slot_table, 'grp', split_axis=0, concat_axis=0, tiled=True)]
    unnamed x10 -> x18, local copies, waits for them, and re-layouts: 2.42 us -> 1.09 us
  transfers between devices with their start and end apart: 4 -> 7, of which waited for: 3 -> 5; matrix products, arithmetic and copies ran while one was open for 16% -> 15% of each run, Pallas kernels for 0% -> 0%
where the time goes in v1:
time: 121 us; the launch traced here: 120 us
  waiting for transfers between devices  39.4 us (33%)
  matrix products  38.1 us (31%)
  starting transfers between devices  19.4 us (16%)
  local copies, waits for them, and re-layouts  17.7 us (15%)
  other arithmetic  5.07 us (4%)
    dot_general x1, matrix products, tile_force(): jnp.dot(geometry[0:3], pressure, precision=lax.Precision.HIGHEST, preferr...  37.2 us
    all_to_all x1, waiting for transfers between devices, shards(): lax.all_to_all(own_forces, 'dom', split_axis=0, concat_axis=0, tiled=True)  15.2 us
    all_to_all x1, waiting for transfers between devices, shards(): lax.all_to_all(outgoing, 'dom', split_axis=0, concat_axis=0, tiled=True)  12.4 us
    ppermute x3, waiting for transfers between devices, turned_line(): parts = [lax.ppermute(parts[0], name, route), *parts]  9.98 us
    gather x2, local copies, waits for them, and re-layouts, shards(): corners = jnp.take(seg_nodes, seg_conn, axis=1)  8.59 us
    all_to_all x1, starting transfers between devices, shards(): lax.all_to_all(seg_table, 'grp', split_axis=0, concat_axis=0, tiled=True)  5.19 us
    all_to_all x1, starting transfers between devices, shards(): lax.all_to_all(outgoing, 'dom', split_axis=0, concat_axis=0, tiled=True)  4.88 us
    all_to_all x1, starting transfers between devices, shards(): lax.all_to_all(own_forces, 'dom', split_axis=0, concat_axis=0, tiled=True)  3.49 us
  transfers between devices with their start and end apart: 7, of which 5 were waited for; matrix products, arithmetic and copies ran while one was open for 15% of the time, Pallas kernels for 0%

profile of v1, /device:TPU:0, one launch (start us, length us, event | category | flops | bytes accessed | tf_op | source)
XLA Modules:
  0.0 120.0 jit_solution(6367158374907877924)
XLA Ops:
  0.0 5.2 %all-to-all-start.1 = ((s32[4,1,32]{2,1,0:T(1,128)}), s32[4,1,32]{2,1,0:T(1,128)S(1)}, u32[]{:S(2)}, u32[]{:S(2)}) async-start(s32[4,1,32]{2,1,0:T(1,128)} %bitcast.90), calls=%async_computation.1 | async-start | bytes 4096 | tf_op jit(solution)/shard_map/all_to_all | solution.py:87
  5.2 0.7 compare_and_fusion
  5.9 0.7 compare_select_fusion
  6.7 0.9 copy.50
  7.6 8.1 %gather_fusion = f32[3072,6]{1,0:T(8,128)S(1)} fusion(f32[6,512]{0,1:T(8,128)S(1)} %copy.50, s32[3072]{0:T(1024)S(1)} %broadcast_clamp_fusion), kind=kCustom, calls=%fused_computation | custom fusion | bytes 159744 | tf_op jit(solution)/shard_map/jit(_take)/gather | solution.py:79
  15.7 0.5 copy.51
  16.3 2.1 %collective-permute-start = (f32[8,9,128]{2,1,0:T(8,128)S(1)}, f32[8,9,128]{2,1,0:T(8,128)S(1)}, u32[]{:S(2)}, u32[]{:S(2)}) collective-permute-start(f32[8,9,128]{2,1,0:T(8,128)S(1)} %maximum_bitcast_fusion), channel_id=1, source_target_pairs={{0,8},{8,16},{16,24},{24,0},{1,9},{9,17},{17,25},{25,1},{2,10},{10... | collective-permute-start | bytes 110600 | tf_op jit(solution)/shard_map/ppermute | solution.py:17
  19.0 0.5 fusion.34
  19.5 3.2 %all-to-all-start = ((s32[4,1,32]{2,1,0:T(1,128)}), s32[4,1,32]{2,1,0:T(1,128)S(1)}, u32[]{:S(2)}, u32[]{:S(2)}) async-start(s32[4,1,32]{2,1,0:T(1,128)} %bitcast.1), calls=%async_computation | async-start | bytes 4096 | tf_op jit(solution)/shard_map/all_to_all | solution.py:88
  22.8 1.4 %copy.58 = f32[256,6,128]{2,1,0:T(8,128)} copy(f32[256,6,128]{2,0,1:T(8,128)S(1)} %fusion.34) | data formatting | bytes 1572864 | tf_op jit(solution)/shard_map/dot_general | solution.py:60
  24.3 0.5 broadcast.129
  24.8 0.7 reduce.10
  25.6 1.8 %all-to-all-done = s32[4,1,32]{2,1,0:T(1,128)S(1)} async-done(((s32[4,1,32]{2,1,0:T(1,128)}), s32[4,1,32]{2,1,0:T(1,128)S(1)}, u32[]{:S(2)}, u32[]{:S(2)}) %all-to-all-start) | async-done | bytes 544 | tf_op jit(solution)/shard_map/all_to_all | solution.py:88
  27.4 4.9 %all-to-all-start.2 = ((f32[256,6,128]{2,1,0:T(8,128)}), f32[256,6,128]{2,1,0:T(8,128)S(1)}, u32[]{:S(2)}, u32[]{:S(2)}) async-start(f32[256,6,128]{2,1,0:T(8,128)} %copy.58), calls=%async_computation.2 | async-start | bytes 2097152 | tf_op jit(solution)/shard_map/all_to_all | solution.py:78
  32.3 0.7 reduce.11
  33.1 0.6 compare_and_fusion.1
  33.7 0.6 collective-permute-start.1
  34.3 4.8 %collective-permute-done.1 = f32[8,9,128]{2,1,0:T(8,128)S(1)} collective-permute-done((f32[8,9,128]{2,1,0:T(8,128)S(1)}, f32[8,9,128]{2,1,0:T(8,128)S(1)}, u32[]{:S(2)}, u32[]{:S(2)}) %collective-permute-start.1) | collective-permute-done | bytes 36896 | tf_op jit(solution)/shard_map/ppermute | solution.py:17
  39.1 5.2 %collective-permute-done.2 = f32[8,9,128]{2,1,0:T(8,128)S(1)} collective-permute-done((f32[8,9,128]{2,1,0:T(8,128)S(1)}, f32[8,9,128]{2,1,0:T(8,128)S(1)}, u32[]{:S(2)}, u32[]{:S(2)}) %collective-permute-start.2) | collective-permute-done | bytes 36896 | tf_op jit(solution)/shard_map/ppermute | solution.py:17
  44.4 0.8 gather_fusion.1
  45.4 1.0 fusion.53
  46.4 12.4 %all-to-all-done.2 = f32[256,6,128]{2,1,0:T(8,128)S(1)} async-done(((f32[256,6,128]{2,1,0:T(8,128)}), f32[256,6,128]{2,1,0:T(8,128)S(1)}, u32[]{:S(2)}, u32[]{:S(2)}) %all-to-all-start.2) | async-done | bytes 786464 | tf_op jit(solution)/shard_map/all_to_all | solution.py:78
  58.8 0.8 gather_fusion.2
  59.6 0.9 broadcast_select_fusion.1
  60.5 0.3 fusion.54
  60.8 37.2 %fusion.14 = f32[128,3,128]{2,1,0:T(4,128)S(1)} fusion(f32[128,128]{1,0:T(8,128)S(1)} %bitcast.74, f32[128,128]{1,0:T(8,128)S(1)} %bitcast.83, f32[128,128]{1,0:T(8,128)S(1)} %bitcast.75, f32[128,128]{1,0:T(8,128)S(1)} %bitcast.76, f32[128,128]{1,0:T(8,128)S(1)} %bitcast.84, f32[128,128]{1,0:T(8,128)S(1)} %bitcast.77, f32[128,128]{1,0:T(8,128)S(1)} %bitcast.78, ...), kind=kOutput, calls=%fused_computation.24 | convolution fusion | flops 134217728 | bytes 1441792 | tf_op jit(solution)/shard_map/vmap()/dot_general | solution.py:50
  98.2 0.3 fusion.37
  98.5 1.1 copy.60
  99.6 3.5 %all-to-all-start.3 = ((f32[256,3,128]{2,1,0:T(4,128)}), f32[256,3,128]{2,1,0:T(4,128)S(1)}, u32[]{:S(2)}, u32[]{:S(2)}) async-start(f32[256,3,128]{2,1,0:T(4,128)} %copy.60), calls=%async_computation.3 | async-start | bytes 1048576 | tf_op jit(solution)/shard_map/all_to_all | solution.py:97
  103.1 15.2 %all-to-all-done.3 = f32[256,3,128]{2,1,0:T(4,128)S(1)} async-done(((f32[256,3,128]{2,1,0:T(4,128)}), f32[256,3,128]{2,1,0:T(4,128)S(1)}, u32[]{:S(2)}, u32[]{:S(2)}) %all-to-all-start.3) | async-done | bytes 393248 | tf_op jit(solution)/shard_map/all_to_all | solution.py:97
  118.4 0.7 gather_fusion.3
  119.3 0.7 copy.61
  (50 shorter events, 1.8 us)
Async XLA Ops:
  0.0 19.5 %all-to-all-start.1 = ((s32[4,1,32]{2,1,0:T(1,128)}), s32[4,1,32]{2,1,0:T(1,128)S(1)}, u32[]{:S(2)}, u32[]{:S(2)}) async-start(s32[4,1,32]{2,1,0:T(1,128)} %bitcast.90), calls=%async_computation.1 | async-start | bytes 4096 | tf_op jit(solution)/shard_map/all_to_all | solution.py:87
  7.5 11.1 %copy-start.4 = (s32[128]{0:T(128)S(1)}, s32[128]{0:T(128)}, u32[]{:S(2)}) copy-start(s32[128]{0:T(128)} %param.7) | copy-start | bytes 1540
  7.6 11.3 %copy-start = (f32[128,6,128]{2,0,1:T(8,128)S(1)}, f32[128,6,128]{2,0,1:T(8,128)}, u32[]{:S(2)}) copy-start(f32[128,6,128]{2,0,1:T(8,128)} %param.6) | copy-start | bytes 1179652
  16.3 17.4 %collective-permute-start = (f32[8,9,128]{2,1,0:T(8,128)S(1)}, f32[8,9,128]{2,1,0:T(8,128)S(1)}, u32[]{:S(2)}, u32[]{:S(2)}) collective-permute-start(f32[8,9,128]{2,1,0:T(8,128)S(1)} %maximum_bitcast_fusion), channel_id=1, source_target_pairs={{0,8},{8,16},{16,24},{24,0},{1,9},{9,17},{17,25},{25,1},{2,10},{10... | collective-permute-start | bytes 110600 | tf_op jit(solution)/shard_map/ppermute | solution.py:17
  19.5 7.8 %all-to-all-start = ((s32[4,1,32]{2,1,0:T(1,128)}), s32[4,1,32]{2,1,0:T(1,128)S(1)}, u32[]{:S(2)}, u32[]{:S(2)}) async-start(s32[4,1,32]{2,1,0:T(1,128)} %bitcast.1), calls=%async_computation | async-start | bytes 4096 | tf_op jit(solution)/shard_map/all_to_all | solution.py:88
  27.4 31.4 %all-to-all-start.2 = ((f32[256,6,128]{2,1,0:T(8,128)}), f32[256,6,128]{2,1,0:T(8,128)S(1)}, u32[]{:S(2)}, u32[]{:S(2)}) async-start(f32[256,6,128]{2,1,0:T(8,128)} %copy.58), calls=%async_computation.2 | async-start | bytes 2097152 | tf_op jit(solution)/shard_map/all_to_all | solution.py:78
  33.7 5.4 %collective-permute-start.1 = (f32[8,9,128]{2,1,0:T(8,128)S(1)}, f32[8,9,128]{2,1,0:T(8,128)S(1)}, u32[]{:S(2)}, u32[]{:S(2)}) collective-permute-start(f32[8,9,128]{2,1,0:T(8,128)S(1)} %collective-permute-done), channel_id=1, source_target_pairs={{0,8},{8,16},{16,24},{24,0},{1,9},{9,17},{17,25},{25,1},{2,10},{10... | collective-permute-start | bytes 110600 | tf_op jit(solution)/shard_map/ppermute | solution.py:17
  39.1 5.2 %collective-permute-start.2 = (f32[8,9,128]{2,1,0:T(8,128)S(1)}, f32[8,9,128]{2,1,0:T(8,128)S(1)}, u32[]{:S(2)}, u32[]{:S(2)}) collective-permute-start(f32[8,9,128]{2,1,0:T(8,128)S(1)} %collective-permute-done.1), channel_id=1, source_target_pairs={{0,8},{8,16},{16,24},{24,0},{1,9},{9,17},{17,25},{25,1},{2,10},{10... | collective-permute-start | bytes 110600 | tf_op jit(solution)/shard_map/ppermute | solution.py:17
  59.6 1.2 %copy-start.1 = (f32[128,1,128]{2,1,0:T(1,128)S(1)}, f32[128,1,128]{2,1,0:T(1,128)}, u32[]{:S(2)}) copy-start(f32[128,1,128]{2,1,0:T(1,128)} %get-tuple-element.13) | copy-start | bytes 196612
  59.6 1.2 %copy-start.2 = (f32[128,1,128]{2,1,0:T(1,128)S(1)}, f32[128,1,128]{2,1,0:T(1,128)}, u32[]{:S(2)}) copy-start(f32[128,1,128]{2,1,0:T(1,128)} %get-tuple-element.14) | copy-start | bytes 196612
  59.6 1.2 %copy-start.3 = (f32[128,1,128]{2,1,0:T(1,128)S(1)}, f32[128,1,128]{2,1,0:T(1,128)}, u32[]{:S(2)}) copy-start(f32[128,1,128]{2,1,0:T(1,128)} %get-tuple-element.15) | copy-start | bytes 196612
  99.6 18.8 %all-to-all-start.3 = ((f32[256,3,128]{2,1,0:T(4,128)}), f32[256,3,128]{2,1,0:T(4,128)S(1)}, u32[]{:S(2)}, u32[]{:S(2)}) async-start(f32[256,3,128]{2,1,0:T(4,128)} %copy.60), calls=%async_computation.3 | async-start | bytes 1048576 | tf_op jit(solution)/shard_map/all_to_all | solution.py:97
